TPU v7x, 128 devices: a whole 4x4x4 slice. The times are simulated.
128 devices in a mesh: dp: 16 (over y, x), row: 2 (over core), col: 4 (over z).
Axes of the slice: x: 4, y: 4, z: 4, core: 2. Of those that a mesh axis runs over, the one named last changes fastest.
Arguments:
- tokens: bfloat16 [15360, 4096], P(('dp', 'col'), 'row'), may hold values from -6 to 6
- hidden_cot: bfloat16 [15360, 14336], P(('dp', 'row'), 'col'), may hold values from -0.048339844 to 0.048339844
- gate_pre: bfloat16 [15360, 14336], P(('dp', 'row'), 'col'), may hold values from -10 to 10
- up_pre: bfloat16 [15360, 14336], P(('dp', 'row'), 'col'), may hold values from -6 to 6
Outputs:
- grad_gate: bfloat16 [2, 2048, 14336], P('row', 'dp', 'col')
All inputs are finite; a program needn't handle non-finite values.
Results may differ from a plain program's by a relative error of at most 0.014.
Values may be sent and summed in bfloat16 or wider, within the bound.
A program may use at most 128 MiB of HBM per device.

v0:
```python
import jax
import jax.numpy as jnp
from jax import lax
from jax.sharding import PartitionSpec as P


def copy_for_each(x, axis):
    copies = jnp.broadcast_to(x, (lax.axis_size(axis), *x.shape))
    return lax.all_to_all(copies, axis, split_axis=0, concat_axis=0, tiled=True)


def in_order(tiles, dim):
    lengths = list(tiles.shape[1:])
    lengths[dim] *= tiles.shape[0]
    return jnp.moveaxis(tiles, 0, dim).reshape(lengths)


def gather_directly(x, axis, dim):
    tiles = copy_for_each(x, axis)
    return in_order(tiles, dim)


def contract_rows(left, right):
    return lax.dot_general(
        left, right, (((0,), (0,)), ((), ())), preferred_element_type=jnp.float32
    )


def on_device(tokens, hidden_cot, gate_pre, up_pre):
    tok_full = lax.all_gather(tokens, "col", axis=0, tiled=True)
    gate_val = gate_pre.astype(jnp.float32)
    up_val = up_pre.astype(jnp.float32)
    cot_val = hidden_cot.astype(jnp.float32)
    sigma = jax.nn.sigmoid(gate_val)
    gate_grad = (cot_val * up_val * sigma * (1.0 + gate_val * (1.0 - sigma))).astype(jnp.bfloat16)
    group_part = contract_rows(tok_full, gather_directly(gate_grad, "row", 0))
    summed = lax.psum_scatter(
        group_part.astype(jnp.bfloat16), "dp", scatter_dimension=0, tiled=True
    )
    return summed.reshape(1, summed.shape[0], summed.shape[1])


def solution(mesh):
    in_specs = (
        P(("dp", "col"), "row"),
        P(("dp", "row"), "col"),
        P(("dp", "row"), "col"),
        P(("dp", "row"), "col"),
    )
    out_specs = P("row", "dp", "col")
    return jax.shard_map(
        on_device, mesh=mesh, in_specs=in_specs, out_specs=out_specs, check_vma=False
    )
```

profile of v0, /device:TPU:1, one launch (start us, length us, event | category | flops | bytes accessed | tf_op | source)
XLA Modules:
  0.0 211.0 jit_solution(15205189420382269202)
XLA Ops:
  6.5 0.0 all-gather.2.cloned.1.call-start
  6.5 0.7 all-gather.2.cloned.1.call-update
  7.3 0.0 reduce-scatter.4.cloned.1.call-start
  7.3 5.6 %fusion.6 = bf16[480,3584]{1,0:T(8,128)(2,1)S(1)} fusion(bf16[480,3584]{1,0:T(8,128)(2,1)} %param.6, bf16[480,3584]{1,0:T(8,128)(2,1)} %param.7, bf16[480,3584]{1,0:T(8,128)(2,1)} %param.5), kind=kLoop, calls=%fused_computation.9 | loop fusion | flops 22364160 | bytes 13762560 | tf_op jit(solution)/shard_map/convert_element_type | solution.py:35
  12.9 0.4 broadcast_in_dim.3
  13.3 11.5 %all_to_all.5 = bf16[2,480,3584]{2,1,0:T(8,128)(2,1)} all-to-all(bf16[2,480,3584]{2,1,0:T(8,128)(2,1)S(1)} %broadcast_in_dim.3), channel_id=1, replica_groups=mesh['dp'=16,'row'=2,'col'=4] {'row'}, dimensions={0} | all-to-all | bytes 13762560 | tf_op jit(solution)/shard_map/all_to_all | solution.py:9
  24.8 33.5 %all-gather.2.cloned.1.call-done = bf16[960,2048]{1,0:T(8,128)(2,1)} async-done(((bf16[240,2048]{1,0:T(8,128)(2,1)}), bf16[960,2048]{1,0:T(8,128)(2,1)}) %all-gather.2.cloned.1.call-update) | async-done | bytes 3932176 | tf_op jit(solution)/shard_map/all_gather | solution.py:30
  58.3 21.9 %fusion = bf16[2048,3584]{0,1:T(8,128)(2,1)} fusion(bf16[960,3584]{1,0:T(8,128)(2,1)} %bitcast.7, bf16[960,2048]{1,0:T(8,128)(2,1)} %all-gather.2.cloned.1.call-done), kind=kOutput, calls=%fused_computation.1 | convolution fusion | flops 14100201472 | bytes 25493504 | tf_op jit(solution)/shard_map/dot_general | solution.py:24
  80.2 18.6 %copy.7 = bf16[2048,3584]{1,0:T(8,128)(2,1)} copy(bf16[2048,3584]{0,1:T(8,128)(2,1)} %fusion) | data formatting | bytes 29360128
  98.8 0.0 reduce-scatter.4.cloned.1.call-update
  98.9 102.5 %reduce-scatter.4.cloned.1.call-done = bf16[128,3584]{1,0:T(8,128)(2,1)} async-done(((bf16[2048,3584]{1,0:T(8,128)(2,1)}), bf16[128,3584]{1,0:T(8,128)(2,1)}) %reduce-scatter.4.cloned.1.call-update) | async-done | bytes 917520
  201.4 1.5 copy.8
  202.9 1.3 copy.6
Async XLA Ops:
  6.5 51.8 %all-gather.2.cloned.1.call-start = ((), (), s32[]{:S(2)}) async-start(), calls=%async_computation.2 | async-start | bytes 4915200 | tf_op jit(solution)/shard_map/all_gather | solution.py:30
  7.3 194.1 %reduce-scatter.4.cloned.1.call-start = ((), (), s32[]{:S(2)}) async-start(), calls=%async_computation.3 | async-start | bytes 15597568
Sparse Core Ops, SparseCore 0:
  9.0 49.2 all-gather.1
  99.0 102.3 reduce-scatter.3
where the time goes:
time: 212 us; the launch traced here: 211 us
  waiting for transfers between devices  137 us (65%)
  local copies, waits for them, and re-layouts  21.9 us (10%)
  matrix products  21.9 us (10%)
  between operations  13.4 us (6%)
  blocking collectives  11.5 us (5%)
  other arithmetic  5.55 us (3%)
    unnamed x3, waiting for transfers between devices  103 us
    all_gather x1, waiting for transfers between devices, on_device(): tok_full = lax.all_gather(tokens, 'col', axis=0, tiled=True)  33.5 us
    dot_general x1, matrix products, contract_rows(): lax.dot_general(left, right, (((0,), (0,)), ((), ())), preferred_element_...  21.9 us
    unnamed x2, local copies, waits for them, and re-layouts  20.2 us
    all_to_all x1, blocking collectives, copy_for_each(): return lax.all_to_all(copies, axis, split_axis=0, concat_axis=0, tiled=True)  11.5 us
    convert_element_type x1, other arithmetic, on_device(): (cot_val * up_val * sigma * (1.0 + gate_val * (1.0 - sigma))).astype(jnp....  5.55 us
  transfers between devices with their start and end apart: 2, of which 2 were waited for; matrix products, arithmetic and copies ran while one was open for 3% of the time, Pallas kernels for 0%

commit v1 on v0

v1 whole, which is shorter than its diff:
```python
import jax
import jax.numpy as jnp
from jax import lax
from jax.experimental import pallas as pl
from jax.experimental.pallas import tpu as pltpu
from jax.sharding import PartitionSpec as P

MESH = pl.DeviceIdType.MESH
SIDE = 4
CORES = 2
DEPTH = 4
ORDER = (
    (2, 2), (2, 1), (2, 3), (1, 2), (3, 2), (2, 0), (0, 2), (1, 1),
    (1, 3), (3, 1), (3, 3), (1, 0), (3, 0), (0, 1), (0, 3), (0, 0),
)
STEP = {2: 0, 1: 1, 3: 2, 0: 3}
FLOWS = 4
FAR, JOINED, DIRECT = 0, 1, 2


def kernel(
    tok_in, cot_in, gate_in, up_in, out,
    tok, tok_t, cot, gate, up, grad, part, inbox, inbox2,
    local_sem, gate_sem, out_sem,
    tok_send, tok_recv, grad_send, grad_recv,
    send1, recv1, send2, recv2,
):
    share, own_rows = tok_in.shape[0], cot_in.shape[0]
    lanes = tok.shape[2]
    width = grad.shape[1] // FLOWS
    dp = lax.axis_index("dp")
    core = lax.axis_index("row")
    z = lax.axis_index("col")
    y, x = lax.div(dp, SIDE), lax.rem(dp, SIDE)

    def shift(index, by):
        return lax.rem(index + by, SIDE)

    def along(axis, by):
        if axis == "x":
            return {"dp": y * SIDE + shift(x, by % SIDE)}
        return {"dp": shift(y, by % SIDE) * SIDE + x}

    z_up, z_down = {"col": shift(z, 1)}, {"col": shift(z, DEPTH - 1)}
    partner = {"row": 1 - core}

    def remote(src, dst, ss, rs, device):
        return pltpu.make_async_remote_copy(
            src_ref=src, dst_ref=dst, send_sem=ss, recv_sem=rs,
            device_id=device, device_id_type=MESH,
        )

    def tok_rows(k, owner):
        rows = pl.ds(pl.multiple_of(owner * share, 16), share)
        return tok.at[k, rows, :]

    def load_tokens(k):
        dy, dx = ORDER[k]
        owner = shift(y, dy) * SIDE + shift(x, dx)
        columns = pl.ds(pl.multiple_of(owner * lanes, lanes), lanes)
        return pltpu.make_async_copy(
            tok_in.at[:, columns], tok_rows(k, z), local_sem.at[k]
        )

    def columns_of(c):
        return slice(c * width, (c + 1) * width)

    def load_gates(c):
        return [
            pltpu.make_async_copy(
                src.at[:, columns_of(c)], dst.at[:, columns_of(c)], gate_sem.at[i, c]
            )
            for i, (src, dst) in enumerate(((cot_in, cot), (gate_in, gate), (up_in, up)))
        ]

    for k in range(4):
        load_tokens(k).start()
    for c in range(FLOWS):
        for copy in load_gates(c):
            copy.start()
    for k in range(4, len(ORDER)):
        load_tokens(k).start()

    neighbours = [partner, z_up, z_down] + [
        along(axis, by) for axis in "xy" for by in (1, -1)
    ]
    barrier = pltpu.get_barrier_semaphore()
    for device in neighbours:
        pl.semaphore_signal(barrier, inc=1, device_id=device, device_id_type=MESH)
    pl.semaphore_wait(barrier, len(neighbours))

    def tok_copy(k, i):
        if i < 2:
            rows, to = tok_rows(k, z), (z_up, z_down)[i]
        elif k % 2 == 0:
            rows, to = tok_rows(k, shift(z, DEPTH - 1)), z_up
        else:
            rows, to = tok_rows(k, shift(z, 1)), z_down
        return remote(rows, rows, tok_send.at[k, i], tok_recv.at[k, i], to)

    def arrival(k, i):
        source = shift(z, (DEPTH - 1, 1, 2)[i])
        rows = tok_rows(k, source)
        return remote(rows, rows, tok_send.at[k, i], tok_recv.at[k, i], z_up)

    def give_tokens(k):
        if k < len(ORDER):
            load_tokens(k).wait()
            tok_copy(k, 0).start()
            tok_copy(k, 1).start()

    def pass_tokens(k):
        if k < len(ORDER):
            arrival(k, k % 2).wait_recv()
            tok_copy(k, 2).start()

    def await_tokens(k):
        arrival(k, 1 - k % 2).wait_recv()
        arrival(k, 2).wait_recv()

    own_offset = pl.multiple_of(core * own_rows, 16)

    def grad_rows(c, offset):
        return grad.at[pl.ds(pl.multiple_of(offset, 16), own_rows), columns_of(c)]

    def grad_copy(c):
        mine = grad_rows(c, own_offset)
        return remote(mine, mine, grad_send.at[c], grad_recv.at[c], partner)

    def grad_arrival(c):
        theirs = grad_rows(c, (1 - core) * own_rows)
        return remote(theirs, theirs, grad_send.at[c], grad_recv.at[c], partner)

    def make_grad(c):
        for copy in load_gates(c):
            copy.wait()

        def rows_of(i, carry):
            rows = pl.ds(pl.multiple_of(i * 16, 16), 16)
            g = gate[rows, columns_of(c)].astype(jnp.float32)
            u = up[rows, columns_of(c)].astype(jnp.float32)
            h = cot[rows, columns_of(c)].astype(jnp.float32)
            s = jax.nn.sigmoid(g)
            there = pl.ds(pl.multiple_of(own_offset + i * 16, 16), 16)
            grad[there, columns_of(c)] = (h * u * s * (1.0 + g * (1.0 - s))).astype(grad.dtype)
            return carry

        lax.fori_loop(0, own_rows // 16, rows_of, 0)
        grad_copy(c).start()

    def axes_of(q):
        return ("x", "y") if q < 2 else ("y", "x")

    def sign_of(q):
        return 1 if q % 2 == 0 else -1

    def block_of(q, first, second):
        offsets = (second % SIDE, first % SIDE) if q < 2 else (first % SIDE, second % SIDE)
        return ORDER.index(offsets)

    def unit(k, q):
        return part.at[k, :, columns_of(q)]

    def copy1(q, role, j, src=None):
        axis, sign = axes_of(q)[0], sign_of(q)
        box = inbox.at[q, role, j]
        device = along(axis, -sign if role == DIRECT else sign)
        return remote(
            box if src is None else src, box,
            send1.at[q, role, j], recv1.at[q, role, j], device,
        )

    def copy2(q, role, src=None):
        axis, sign = axes_of(q)[1], sign_of(q)
        box = inbox2.at[q, role]
        device = along(axis, -sign if role == DIRECT else sign)
        return remote(
            box if src is None else src, box,
            send2.at[q, role], recv2.at[q, role], device,
        )

    def add_into(dst, *terms):
        rows_all = dst.shape[0]

        def rows_of(i, carry):
            rows = pl.ds(pl.multiple_of(i * 16, 16), 16)
            total = dst[rows, :].astype(jnp.float32)
            for term in terms:
                total = total + term[rows, :].astype(jnp.float32)
            dst[rows, :] = total.astype(dst.dtype)
            return carry

        lax.fori_loop(0, rows_all // 16, rows_of, 0)

    def send_first(k, q):
        dy, dx = ORDER[k]
        first, second = (dx, dy) if q < 2 else (dy, dx)
        sign = sign_of(q)
        if first == 2:
            role = FAR
        elif first == -sign % SIDE:
            role = DIRECT
        else:
            return
        copy1(q, role, STEP[second], unit(k, q)).start()

    def join(q, second):
        j = STEP[second % SIDE]
        mine = unit(block_of(q, sign_of(q), second), q)
        copy1(q, FAR, j).wait_recv()
        add_into(mine, inbox.at[q, FAR, j])
        copy1(q, JOINED, j, mine).start()

    def settle(q, second, *more):
        j = STEP[second % SIDE]
        mine = unit(block_of(q, 0, second), q)
        copy1(q, JOINED, j).wait_recv()
        copy1(q, DIRECT, j).wait_recv()
        add_into(mine, inbox.at[q, JOINED, j], inbox.at[q, DIRECT, j], *more)
        return mine

    def far_second(q):
        copy2(q, FAR, settle(q, 2)).start()

    def direct_second(q):
        copy2(q, DIRECT, settle(q, -sign_of(q))).start()

    def join_second(q):
        copy2(q, FAR).wait_recv()
        mine = settle(q, sign_of(q), inbox2.at[q, FAR])
        copy2(q, JOINED, mine).start()

    def write(q):
        return pltpu.make_async_copy(
            unit(block_of(q, 0, 0), q), out.at[0, :, columns_of(q)], out_sem.at[q]
        )

    def finish(q):
        copy2(q, JOINED).wait_recv()
        copy2(q, DIRECT).wait_recv()
        settle(q, 0, inbox2.at[q, JOINED], inbox2.at[q, DIRECT])
        write(q).start()

    flows = range(FLOWS)

    def after(k):
        if k == 5:
            for q in flows:
                join(q, 2)
        elif k == 9:
            for q in flows:
                join(q, 1)
        elif k == 11:
            for q in flows:
                join(q, 3)
        elif k == 14:
            for q in flows:
                far_second(q)

    give_tokens(0)
    give_tokens(1)
    make_grad(0)
    make_grad(1)
    pass_tokens(0)
    give_tokens(2)
    make_grad(2)
    pass_tokens(1)
    give_tokens(3)
    make_grad(3)
    pass_tokens(2)
    give_tokens(4)

    half = 2 * width

    def block(b, carry):
        for k in range(len(ORDER)):

            @pl.when(b == k)
            def _(k=k):
                pass_tokens(k + 3)
                give_tokens(k + 5)
                await_tokens(k)
                if k == 0:
                    for c in flows:
                        grad_arrival(c).wait_recv()

        tok_t[...] = tok[b].T
        for pair in range(2):
            part[b, :, pair * half:(pair + 1) * half] = jnp.dot(
                tok_t[...], grad[:, pair * half:(pair + 1) * half],
                preferred_element_type=jnp.float32,
            ).astype(part.dtype)
            for k in range(len(ORDER)):

                @pl.when(b == k)
                def _(k=k, pair=pair):
                    send_first(k, 2 * pair)
                    send_first(k, 2 * pair + 1)
                    if pair == 1:
                        after(k)

        return carry

    lax.fori_loop(0, len(ORDER), block, 0)

    for q in flows:
        join(q, 0)
    for q in flows:
        direct_second(q)
    for q in flows:
        join_second(q)
    for q in flows:
        finish(q)

    for k in range(len(ORDER)):
        for i in range(3):
            tok_copy(k, i).wait_send()
    for c in flows:
        grad_copy(c).wait_send()
    for q in flows:
        for role in (FAR, JOINED, DIRECT):
            for j in range(SIDE):
                copy1(q, role, j).wait_send()
            copy2(q, role).wait_send()
    for q in flows:
        write(q).wait()


def on_device(tokens, hidden_cot, gate_pre, up_pre):
    share, model = tokens.shape
    own_rows, hidden = hidden_cot.shape
    lanes = model // len(ORDER)
    width = hidden // FLOWS
    dtype = tokens.dtype
    dma = pltpu.SemaphoreType.DMA
    any_space = pl.BlockSpec(memory_space=pl.ANY)
    return pl.pallas_call(
        kernel,
        out_shape=jax.ShapeDtypeStruct((1, lanes, hidden), dtype),
        in_specs=[any_space] * 4,
        out_specs=any_space,
        scratch_shapes=[
            pltpu.VMEM((len(ORDER), DEPTH * share, lanes), dtype),
            pltpu.VMEM((lanes, DEPTH * share), dtype),
            pltpu.VMEM((own_rows, hidden), dtype),
            pltpu.VMEM((own_rows, hidden), dtype),
            pltpu.VMEM((own_rows, hidden), dtype),
            pltpu.VMEM((CORES * own_rows, hidden), dtype),
            pltpu.VMEM((len(ORDER), lanes, hidden), dtype),
            pltpu.VMEM((FLOWS, 3, SIDE, lanes, width), dtype),
            pltpu.VMEM((FLOWS, 3, lanes, width), dtype),
            dma((len(ORDER),)),
            dma((3, FLOWS)),
            dma((FLOWS,)),
            dma((len(ORDER), 3)),
            dma((len(ORDER), 3)),
            dma((FLOWS,)),
            dma((FLOWS,)),
            dma((FLOWS, 3, SIDE)),
            dma((FLOWS, 3, SIDE)),
            dma((FLOWS, 3)),
            dma((FLOWS, 3)),
        ],
        compiler_params=pltpu.CompilerParams(
            collective_id=0, has_side_effects=True, vmem_limit_bytes=62 * 2**20
        ),
    )(tokens, hidden_cot, gate_pre, up_pre)


def solution(mesh):
    in_specs = (
        P(("dp", "col"), "row"),
        P(("dp", "row"), "col"),
        P(("dp", "row"), "col"),
        P(("dp", "row"), "col"),
    )
    out_specs = P("row", "dp", "col")
    return jax.shard_map(
        on_device, mesh=mesh, in_specs=in_specs, out_specs=out_specs, check_vma=False
    )
```

time: 212 us -> 99.6 us (0.47)
  waiting for transfers between devices: 137 us -> 0 us
  Pallas kernels: 0 us -> 97.3 us
  matrix products: 21.9 us -> 0 us
  local copies, waits for them, and re-layouts: 21.9 us -> 2.16 us
  between operations: 13.4 us -> 0.01 us
  blocking collectives: 11.5 us -> 0 us
  other arithmetic: 5.55 us -> 0 us
    unnamed x3 -> x0, waiting for transfers between devices: 103 us -> none
    pallas_call x0 -> x1, Pallas kernels: none -> 97.3 us  [on_device(): pl.pallas_call(kernel, out_shape=jax.ShapeDtypeStruct((1, lanes, hidden),...]
    all_gather x1 -> x0, waiting for transfers between devices: 33.5 us -> none  [on_device(): tok_full = lax.all_gather(tokens, 'col', axis=0, tiled=True)]
    dot_general x1 -> x0, matrix products: 21.9 us -> none  [contract_rows(): lax.dot_general(left, right, (((0,), (0,)), ((), ())), preferred_element_...]
    unnamed x2 -> x1, local copies, waits for them, and re-layouts: 20.2 us -> 2.16 us
    all_to_all x1 -> x0, blocking collectives: 11.5 us -> none  [copy_for_each(): return lax.all_to_all(copies, axis, split_axis=0, concat_axis=0, tiled=True)]
    convert_element_type x1 -> x0, other arithmetic: 5.55 us -> none  [on_device(): (cot_val * up_val * sigma * (1.0 + gate_val * (1.0 - sigma))).astype(jnp....]
  transfers between devices with their start and end apart: 2 -> 0, of which waited for: 2 -> 0; matrix products, arithmetic and copies ran while one was open for 3% -> 0% of each run, Pallas kernels for 0% -> 0%
where the time goes in v1:
time: 99.6 us; the launch traced here: 99.4 us
  Pallas kernels  97.3 us (98%)
  local copies, waits for them, and re-layouts  2.16 us (2%)
    pallas_call x1, Pallas kernels, on_device(): pl.pallas_call(kernel, out_shape=jax.ShapeDtypeStruct((1, lanes, hidden),...  97.3 us
    unnamed x1, local copies, waits for them, and re-layouts  2.16 us

profile of v1, /device:TPU:1, one launch (start us, length us, event | category | flops | bytes accessed | tf_op | source)
XLA Modules:
  0.0 99.4 jit_solution(14419271081451565179)
XLA Ops:
  0.0 97.3 %shard_map.46 = bf16[1,128,3584]{2,1,0:T(8,128)(2,1)} custom-call(bf16[240,2048]{1,0:T(8,128)(2,1)} %tok_in.1, bf16[480,3584]{1,0:T(8,128)(2,1)} %cot_in.1, bf16[480,3584]{1,0:T(8,128)(2,1)} %gate_in.1, bf16[480,3584]{1,0:T(8,128)(2,1)} %up_in.1), custom_call_target="tpu_custom_call" | custom-call | tf_op jit(solution)/shard_map/pallas_call | solution.py:337
  97.3 2.2 %copy.6 = bf16[1,128,3584]{2,1,0:T(8,128)(2,1)} copy(bf16[1,128,3584]{2,1,0:T(8,128)(2,1)} %shard_map.46) | data formatting | bytes 1835008

commit v2 on v1

v2 whole, which is shorter than its diff:
```python
import jax
import jax.numpy as jnp
from jax import lax
from jax.experimental import pallas as pl
from jax.experimental.pallas import tpu as pltpu
from jax.sharding import PartitionSpec as P

MESH = pl.DeviceIdType.MESH
SIDE = 4
CORES = 2
DEPTH = 4
ORDER = (
    (2, 2), (2, 1), (2, 3), (1, 2), (3, 2), (2, 0), (0, 2), (1, 1),
    (1, 3), (3, 1), (3, 3), (1, 0), (3, 0), (0, 1), (0, 3), (0, 0),
)
STEP = {2: 0, 1: 1, 3: 2, 0: 3}
FLOWS = 4
FAR, JOINED, DIRECT = 0, 1, 2
GROUPS = ((0, 1), (1, 2), (2, 4), (4, 8), (8, 16))


def kernel(
    tok_in, cot_in, gate_in, up_in, out,
    tok, tok_t, gates, grad, part, inbox, inbox2,
    local_sem, gate_sem, out_sem,
    tok_send, tok_recv, grad_send, grad_recv,
    send1, far1, near1, send2, far2, near2,
):
    share, own_rows = tok_in.shape[0], cot_in.shape[0]
    lanes = tok.shape[2]
    width = grad.shape[1] // FLOWS
    dp = lax.axis_index("dp")
    core = lax.axis_index("row")
    z = lax.axis_index("col")
    y, x = lax.div(dp, SIDE), lax.rem(dp, SIDE)

    def shift(index, by):
        return lax.rem(index + by, SIDE)

    def along(axis, by):
        if axis == "x":
            return {"dp": y * SIDE + shift(x, by % SIDE)}
        return {"dp": shift(y, by % SIDE) * SIDE + x}

    z_up, z_down = {"col": shift(z, 1)}, {"col": shift(z, DEPTH - 1)}
    z_across = {"col": shift(z, 2)}
    partner = {"row": 1 - core}

    def remote(src, dst, ss, rs, device):
        return pltpu.make_async_remote_copy(
            src_ref=src, dst_ref=dst, send_sem=ss, recv_sem=rs,
            device_id=device, device_id_type=MESH,
        )

    def tok_rows(k, owner):
        rows = pl.ds(pl.multiple_of(owner * share, 16), share)
        return tok.at[k, rows, :]

    def group_of(k):
        return next(i for i, (first, end) in enumerate(GROUPS) if first <= k < end)

    def load_tokens(k):
        dy, dx = ORDER[k]
        owner = shift(y, dy) * SIDE + shift(x, dx)
        columns = pl.ds(pl.multiple_of(owner * lanes, lanes), lanes)
        return pltpu.make_async_copy(
            tok_in.at[:, columns], tok_rows(k, z), local_sem.at[group_of(k)]
        )

    def columns_of(c):
        return slice(c * width, (c + 1) * width)

    def load_gates(c):
        for i, src in enumerate((cot_in, gate_in, up_in)):
            pltpu.make_async_copy(
                src.at[:, columns_of(c)], gates.at[i, :, columns_of(c)], gate_sem.at[c]
            ).start()

    def wait_for(ref, sem):
        pltpu.make_async_copy(ref, ref, sem).wait()

    for k in range(4):
        load_tokens(k).start()
    for c in range(FLOWS):
        load_gates(c)
    for k in range(4, len(ORDER)):
        load_tokens(k).start()

    neighbours = [partner, z_up, z_down, z_across] + [
        along(axis, by) for axis in "xy" for by in (1, -1)
    ]
    barrier = pltpu.get_barrier_semaphore()
    for device in neighbours:
        pl.semaphore_signal(barrier, inc=1, device_id=device, device_id_type=MESH)
    pl.semaphore_wait(barrier, len(neighbours))

    def tok_copy(k, i):
        if i < 2:
            rows, to = tok_rows(k, z), (z_up, z_down)[i]
        elif k == 0:
            rows, to = tok_rows(k, z), z_across
        elif k % 2 == 0:
            rows, to = tok_rows(k, shift(z, DEPTH - 1)), z_up
        else:
            rows, to = tok_rows(k, shift(z, 1)), z_down
        return remote(rows, rows, tok_send, tok_recv.at[k, 0 if i == k % 2 else 1], to)

    def give_tokens(k):
        if k < len(ORDER):
            first, end = GROUPS[group_of(k)]
            if k == first:
                rows = pl.ds(pl.multiple_of(z * share, 16), share)
                wait_for(tok.at[first:end, rows, :], local_sem.at[group_of(k)])
            tok_copy(k, 0).start()
            tok_copy(k, 1).start()
            if k == 0:
                tok_copy(k, 2).start()

    def pass_tokens(k):
        if k < len(ORDER):
            wait_for(tok_rows(k, shift(z, (DEPTH - 1, 1)[k % 2])), tok_recv.at[k, 0])
            tok_copy(k, 2).start()

    def await_tokens(k):
        if k == 0:
            wait_for(tok_rows(k, shift(z, DEPTH - 1)), tok_recv.at[k, 0])
        wait_for(tok.at[k, :2 * share, :], tok_recv.at[k, 1])

    own_offset = pl.multiple_of(core * own_rows, 16)

    def grad_rows(c, offset):
        return grad.at[pl.ds(pl.multiple_of(offset, 16), own_rows), columns_of(c)]

    def grad_copy(c):
        mine = grad_rows(c, own_offset)
        return remote(mine, mine, grad_send, grad_recv.at[c], partner)

    def await_grad(c):
        wait_for(grad_rows(c, (1 - core) * own_rows), grad_recv.at[c])

    def make_grad(c):
        wait_for(gates.at[:, :, columns_of(c)], gate_sem.at[c])

        def rows_of(n, carry):
            rows = pl.ds(pl.multiple_of(n * 16, 16), 16)
            h, g, u = (gates[i, rows, columns_of(c)].astype(jnp.float32) for i in range(3))
            s = jax.nn.sigmoid(g)
            there = pl.ds(pl.multiple_of(own_offset + n * 16, 16), 16)
            grad[there, columns_of(c)] = (h * u * s * (1.0 + g * (1.0 - s))).astype(grad.dtype)
            return carry

        lax.fori_loop(0, own_rows // 16, rows_of, 0)
        grad_copy(c).start()

    def axes_of(q):
        return ("x", "y") if q < 2 else ("y", "x")

    def sign_of(q):
        return 1 if q % 2 == 0 else -1

    def block_of(q, first, second):
        offsets = (second % SIDE, first % SIDE) if q < 2 else (first % SIDE, second % SIDE)
        return ORDER.index(offsets)

    def unit(k, q):
        return part.at[k, :, columns_of(q)]

    def send1_to(q, role, j, src):
        axis, sign = axes_of(q)[0], sign_of(q)
        arrived = far1.at[q, j] if role == FAR else near1.at[q, j]
        device = along(axis, -sign if role == DIRECT else sign)
        remote(src, inbox.at[q, role, j], send1, arrived, device).start()

    def send2_to(q, role, src):
        axis, sign = axes_of(q)[1], sign_of(q)
        arrived = far2.at[q] if role == FAR else near2.at[q]
        device = along(axis, -sign if role == DIRECT else sign)
        remote(src, inbox2.at[q, role], send2, arrived, device).start()

    def add_into(dst, *terms):
        rows_all = dst.shape[0]

        def rows_of(i, carry):
            rows = pl.ds(pl.multiple_of(i * 16, 16), 16)
            total = dst[rows, :].astype(jnp.float32)
            for term in terms:
                total = total + term[rows, :].astype(jnp.float32)
            dst[rows, :] = total.astype(dst.dtype)
            return carry

        lax.fori_loop(0, rows_all // 16, rows_of, 0)

    def send_first(k, q):
        dy, dx = ORDER[k]
        first, second = (dx, dy) if q < 2 else (dy, dx)
        sign = sign_of(q)
        if first == 2:
            role = FAR
        elif first == -sign % SIDE:
            role = DIRECT
        else:
            return
        send1_to(q, role, STEP[second], unit(k, q))

    def join(q, second):
        j = STEP[second % SIDE]
        mine = unit(block_of(q, sign_of(q), second), q)
        wait_for(inbox.at[q, FAR, j], far1.at[q, j])
        add_into(mine, inbox.at[q, FAR, j])
        send1_to(q, JOINED, j, mine)

    def settle(q, second, *more):
        j = STEP[second % SIDE]
        mine = unit(block_of(q, 0, second), q)
        wait_for(inbox.at[q, JOINED:, j], near1.at[q, j])
        add_into(mine, inbox.at[q, JOINED, j], inbox.at[q, DIRECT, j], *more)
        return mine

    def far_second(q):
        send2_to(q, FAR, settle(q, 2))

    def direct_second(q):
        send2_to(q, DIRECT, settle(q, -sign_of(q)))

    def join_second(q):
        wait_for(inbox2.at[q, FAR], far2.at[q])
        send2_to(q, JOINED, settle(q, sign_of(q), inbox2.at[q, FAR]))

    def write(q):
        mine = unit(block_of(q, 0, 0), q)
        pltpu.make_async_copy(mine, out.at[0, :, columns_of(q)], out_sem).start()

    def finish(q):
        wait_for(inbox2.at[q, JOINED:], near2.at[q])
        settle(q, 0, inbox2.at[q, JOINED], inbox2.at[q, DIRECT])
        write(q)

    flows = range(FLOWS)

    def after(k):
        if k == 5:
            for q in flows:
                join(q, 2)
        elif k == 9:
            for q in flows:
                join(q, 1)
        elif k == 11:
            for q in flows:
                join(q, 3)
        elif k == 14:
            for q in flows:
                far_second(q)

    def multiply(b, columns):
        part[b, :, columns] = jnp.dot(
            tok_t[...], grad[:, columns], preferred_element_type=jnp.float32
        ).astype(part.dtype)

    give_tokens(0)
    give_tokens(1)
    make_grad(0)
    give_tokens(2)
    make_grad(1)
    make_grad(2)
    give_tokens(3)
    make_grad(3)
    await_tokens(0)
    tok_t[...] = tok[0].T
    for q in flows:
        await_grad(q)
        multiply(0, columns_of(q))
        send_first(0, q)
        if q == 1:
            pass_tokens(1)
            give_tokens(4)
    pass_tokens(2)
    give_tokens(5)

    half = 2 * width

    def block(b, carry):
        for k in range(1, len(ORDER)):

            @pl.when(b == k)
            def _(k=k):
                pass_tokens(k + 2)
                give_tokens(k + 5)
                await_tokens(k)

        tok_t[...] = tok[b].T
        for pair in range(2):
            multiply(b, slice(pair * half, (pair + 1) * half))
            for k in range(1, len(ORDER)):

                @pl.when(b == k)
                def _(k=k, pair=pair):
                    send_first(k, 2 * pair)
                    send_first(k, 2 * pair + 1)
                    if pair == 1:
                        after(k)

        return carry

    lax.fori_loop(1, len(ORDER), block, 0)

    for q in flows:
        join(q, 0)
    for q in flows:
        direct_second(q)
    for q in flows:
        join_second(q)
    for q in flows:
        finish(q)

    wait_for(tok.at[:, :3 * share, :], tok_send)
    wait_for(gates.at[0], grad_send)
    wait_for(inbox, send1)
    wait_for(inbox2, send2)
    wait_for(part.at[0], out_sem)


def on_device(tokens, hidden_cot, gate_pre, up_pre):
    share, model = tokens.shape
    own_rows, hidden = hidden_cot.shape
    lanes = model // len(ORDER)
    width = hidden // FLOWS
    dtype = tokens.dtype
    dma = pltpu.SemaphoreType.DMA
    any_space = pl.BlockSpec(memory_space=pl.ANY)
    return pl.pallas_call(
        kernel,
        out_shape=jax.ShapeDtypeStruct((1, lanes, hidden), dtype),
        in_specs=[any_space] * 4,
        out_specs=any_space,
        scratch_shapes=[
            pltpu.VMEM((len(ORDER), DEPTH * share, lanes), dtype),
            pltpu.VMEM((lanes, DEPTH * share), dtype),
            pltpu.VMEM((3, own_rows, hidden), dtype),
            pltpu.VMEM((CORES * own_rows, hidden), dtype),
            pltpu.VMEM((len(ORDER), lanes, hidden), dtype),
            pltpu.VMEM((FLOWS, 3, SIDE, lanes, width), dtype),
            pltpu.VMEM((FLOWS, 3, lanes, width), dtype),
            dma((len(GROUPS),)),
            dma((FLOWS,)),
            dma,
            dma,
            dma((len(ORDER), 2)),
            dma,
            dma((FLOWS,)),
            dma,
            dma((FLOWS, SIDE)),
            dma((FLOWS, SIDE)),
            dma,
            dma((FLOWS,)),
            dma((FLOWS,)),
        ],
        compiler_params=pltpu.CompilerParams(
            collective_id=0, has_side_effects=True, vmem_limit_bytes=53 * 2**20
        ),
    )(tokens, hidden_cot, gate_pre, up_pre)


def solution(mesh):
    in_specs = (
        P(("dp", "col"), "row"),
        P(("dp", "row"), "col"),
        P(("dp", "row"), "col"),
        P(("dp", "row"), "col"),
    )
    out_specs = P("row", "dp", "col")
    return jax.shard_map(
        on_device, mesh=mesh, in_specs=in_specs, out_specs=out_specs, check_vma=False
    )
```

time: 99.6 us -> 91.1 us (0.915); the launches traced: 99.4 us -> 89.5 us
  Pallas kernels: 97.3 us -> 88.5 us
  local copies, waits for them, and re-layouts: 2.16 us -> 0.93 us
    pallas_call x1, Pallas kernels: 97.3 us -> 88.5 us  [on_device(): pl.pallas_call(kernel, out_shape=jax.ShapeDtypeStruct((1, lanes, hidden),...]
    unnamed x1, local copies, waits for them, and re-layouts: 2.16 us -> 0.93 us
where the time goes in v2:
time: 91.1 us; the launch traced here: 89.5 us
  Pallas kernels  88.5 us (97%)
  local copies, waits for them, and re-layouts  0.93 us (1%)
    pallas_call x1, Pallas kernels, on_device(): pl.pallas_call(kernel, out_shape=jax.ShapeDtypeStruct((1, lanes, hidden),...  88.5 us

profile of v2, /device:TPU:1, one launch (start us, length us, event | category | flops | bytes accessed | tf_op | source)
XLA Modules:
  0.0 89.5 jit_solution(10560452543354816216)
XLA Ops:
  0.0 88.5 %shard_map.46 = bf16[1,128,3584]{2,1,0:T(8,128)(2,1)S(1)} custom-call(bf16[240,2048]{1,0:T(8,128)(2,1)} %tok_in.1, bf16[480,3584]{1,0:T(8,128)(2,1)} %cot_in.1, bf16[480,3584]{1,0:T(8,128)(2,1)} %gate_in.1, bf16[480,3584]{1,0:T(8,128)(2,1)} %up_in.1), custom_call_target="tpu_custom_call" | custom-call | tf_op jit(solution)/shard_map/pallas_call | solution.py:330
  88.5 0.9 %copy.6 = bf16[1,128,3584]{2,1,0:T(8,128)(2,1)} copy(bf16[1,128,3584]{2,1,0:T(8,128)(2,1)S(1)} %shard_map.46) | data formatting | bytes 1835008
